TPU v7x, 32 devices: a whole 2x2x4 slice. The times are simulated.
32 devices in a mesh: win: 4 (over z), slab: 8 (over y, x, core).
Axes of the slice: x: 2, y: 2, z: 4, core: 2. Of those that a mesh axis runs over, the one named last changes fastest.
Arguments:
- lambdas: float32 [16], P('win'), parts along dimension 0, may hold values from 0 to 1
- charge_a: float32 [16, 4096], P('win', 'slab'), parts along dimension 0, may hold values from -3 to 3
- charge_b: float32 [16, 4096], P('win', 'slab'), parts along dimension 0, may hold values from -3 to 3
- perturbed: int32 [16, 4096], P('win', 'slab'), parts along dimension 0, may hold values 0 or 1
- grid_index: int32 [3, 16, 4096], P(None, 'win', 'slab'), parts along dimension 1, may hold values from 0 to 127, as said below
- spline_weights: float32 [3, 4, 16, 4096], P(None, None, 'win', 'slab'), parts along dimension 2, may hold values from 0 to 1, as said below
- spline_slopes: float32 [3, 4, 16, 4096], P(None, None, 'win', 'slab'), parts along dimension 2, may hold values from -1 to 1, as said below
Outputs:
- forces: float32 [3, 16, 4096], P(None, 'win', 'slab'), parts along dimension 1
- energy: float32 [16], P('win'), parts along dimension 0
- lambda_slope: float32 [16], P('win'), parts along dimension 0
There are 4 independent parts, one for each index of `win`. A program takes and returns all parts, laid end to end along the dimension named above; each array names one. Nothing has to cross between parts.
Inputs may be any that keep to these rules, and one draw needn't show every extreme that they name: `grid_index`: the z index of atom i lies in the planes of the slab index that holds it: from (i // 512) * 16 to that plus 16 - 1. `spline_weights`: along each dimension the four weights are the cubic B-spline values (1-u)^3/6, (3u^3-6u^2+4)/6, (-3u^3+3u^2+3u+1)/6, u^3/6 of the atom's fractional offset u in [0, 1). `spline_slopes`: the derivatives in u of spline_weights at the same offsets.
All inputs are finite; a program needn't handle non-finite values. No bound on the sum of `perturbed` on one device may be relied on, other than what follows from the above.
Results may differ from a plain program's by a relative error of at most 0.0003.
Values sent between devices are 32-bit elements; how exact they have to be, the bound alone decides.
A program may use at most 64 MiB of HBM per device.

v0:
```python
import math
import jax
import jax.numpy as jnp
from jax import lax
from jax.sharding import PartitionSpec as P

NX = 128
NY = 128
NZ = 128
highest = lax.Precision.HIGHEST
gauss_width = 2.0


def passed_along(value, axis, steps):
    count = lax.axis_size(axis)
    pairs = [(source, (source + steps) % count) for source in range(count)]
    return lax.ppermute(value, axis, pairs)


def dft_tables(length):
    counter = jnp.arange(length, dtype=jnp.int32)
    product = counter[:, None] * counter[None, :] % length
    angles = product.astype(jnp.float32) * (2.0 * math.pi / length)
    return (jnp.cos(angles), jnp.sin(angles))


def frequency(counter, length):
    return jnp.where(counter >= length // 2, counter - length, counter).astype(jnp.float32) / length


def stencil_table(first_cell, weights, length):
    grid_cells = jnp.arange(length, dtype=jnp.int32)
    matrix = jnp.zeros((first_cell.shape[0], length), jnp.float32)
    for offset in range(4):
        target = (first_cell + offset) % length
        matrix = matrix + weights[offset][:, None] * (
            grid_cells[None, :] == target[:, None]
        ).astype(jnp.float32)
    return matrix


def plane_table(first_cell, weights, plane_count):
    planes = jnp.arange(plane_count, dtype=jnp.int32)
    matrix = jnp.zeros((plane_count, first_cell.shape[0]), jnp.float32)
    for offset in range(4):
        matrix = matrix + weights[offset][None, :] * (
            planes[:, None] == (first_cell + offset)[None, :]
        ).astype(jnp.float32)
    return matrix


def spread_block(charge, cell_index, weights, first_plane, plane_count):
    rows_x = stencil_table(cell_index[0], weights[0], NX)
    rows_y = stencil_table(cell_index[1], weights[1], NY)
    depth_table = plane_table(cell_index[2] - first_plane, weights[2], plane_count)
    right_side = (depth_table * charge[None, :]).T[:, :, None] * rows_y[:, None, :]
    return jnp.einsum("ia,ipb->pab", rows_x, right_side, precision=highest)


def sample_block(
    charge, charge_step, cell_index, weights, slopes, values, first_plane, plane_count
):
    rows_x = stencil_table(cell_index[0], weights[0], NX)
    steep_x = stencil_table(cell_index[0], slopes[0], NX)
    rows_y = stencil_table(cell_index[1], weights[1], NY)
    steep_y = stencil_table(cell_index[1], slopes[1], NY)
    depth_table = plane_table(cell_index[2] - first_plane, weights[2], plane_count)
    steep_z = plane_table(cell_index[2] - first_plane, slopes[2], plane_count)
    along_rows = jnp.einsum("pab,ib->ipa", values, rows_y, precision=highest)
    reduced = jnp.einsum("ia,ipa->ip", rows_x, along_rows, precision=highest)
    reduced_dx = jnp.einsum("ia,ipa->ip", steep_x, along_rows, precision=highest)
    along_steep = jnp.einsum("pab,ib->ipa", values, steep_y, precision=highest)
    reduced_dy = jnp.einsum("ia,ipa->ip", rows_x, along_steep, precision=highest)
    sampled = jnp.einsum("pi,ip->i", depth_table, reduced, precision=highest)
    force_x = -charge * jnp.einsum("pi,ip->i", depth_table, reduced_dx, precision=highest)
    force_y = -charge * jnp.einsum("pi,ip->i", depth_table, reduced_dy, precision=highest)
    force_z = -charge * jnp.einsum("pi,ip->i", steep_z, reduced, precision=highest)
    return (jnp.stack([force_x, force_y, force_z]), jnp.sum(charge_step * sampled))


def xy_forward(owned_grid, planar):
    cosine_x, sine_x, cosine_y, sine_y = planar
    part_real = jnp.einsum("ka,wpab->wpkb", cosine_x, owned_grid, precision=highest)
    part_imaginary = -jnp.einsum("ka,wpab->wpkb", sine_x, owned_grid, precision=highest)
    plane_real = jnp.einsum("wpkb,bl->wpkl", part_real, cosine_y, precision=highest) + jnp.einsum(
        "wpkb,bl->wpkl", part_imaginary, sine_y, precision=highest
    )
    plane_imaginary = jnp.einsum(
        "wpkb,bl->wpkl", part_imaginary, cosine_y, precision=highest
    ) - jnp.einsum("wpkb,bl->wpkl", part_real, sine_y, precision=highest)
    return jnp.stack([plane_real, plane_imaginary], axis=1)


def xy_inverse(slab_values, planar):
    cosine_x, sine_x, cosine_y, sine_y = planar
    value_real = slab_values[:, 0]
    value_imaginary = slab_values[:, 1]
    half_real = jnp.einsum("wpkl,lb->wpkb", value_real, cosine_y, precision=highest) - jnp.einsum(
        "wpkl,lb->wpkb", value_imaginary, sine_y, precision=highest
    )
    half_imaginary = jnp.einsum(
        "wpkl,lb->wpkb", value_imaginary, cosine_y, precision=highest
    ) + jnp.einsum("wpkl,lb->wpkb", value_real, sine_y, precision=highest)
    return jnp.einsum("ak,wpkb->wpab", cosine_x, half_real, precision=highest) - jnp.einsum(
        "ak,wpkb->wpab", sine_x, half_imaginary, precision=highest
    )


def influence_block(first_column, column_count):
    freq_z = frequency(jnp.arange(NZ, dtype=jnp.int32), NZ)[:, None, None]
    freq_x = frequency(first_column + jnp.arange(column_count, dtype=jnp.int32), NX)[None, :, None]
    freq_y = frequency(jnp.arange(NY, dtype=jnp.int32), NY)[None, None, :]
    squared = freq_z * freq_z + freq_x * freq_x + freq_y * freq_y
    positive = squared > 0
    safe_value = jnp.where(positive, squared, jnp.float32(1.0))
    return jnp.where(
        positive,
        jnp.exp(-gauss_width * squared) / (math.pi * NX * NY * NZ * safe_value),
        jnp.float32(0.0),
    )


def column_transform(columns, influence, cosine_z, sine_z):
    column_real = columns[:, 0]
    column_imaginary = columns[:, 1]
    depth_real = jnp.einsum("kz,nzab->nkab", cosine_z, column_real, precision=highest) + jnp.einsum(
        "kz,nzab->nkab", sine_z, column_imaginary, precision=highest
    )
    depth_imaginary = jnp.einsum(
        "kz,nzab->nkab", cosine_z, column_imaginary, precision=highest
    ) - jnp.einsum("kz,nzab->nkab", sine_z, column_real, precision=highest)
    energy_part = 0.5 * jnp.sum(
        influence * (depth_real * depth_real + depth_imaginary * depth_imaginary), axis=(1, 2, 3)
    )
    scaled_real = influence * depth_real
    scaled_imaginary = influence * depth_imaginary
    back_real = jnp.einsum("zk,nkab->nzab", cosine_z, scaled_real, precision=highest) - jnp.einsum(
        "zk,nkab->nzab", sine_z, scaled_imaginary, precision=highest
    )
    back_imaginary = jnp.einsum(
        "zk,nkab->nzab", cosine_z, scaled_imaginary, precision=highest
    ) + jnp.einsum("zk,nkab->nzab", sine_z, scaled_real, precision=highest)
    return (jnp.stack([back_real, back_imaginary], axis=1), energy_part)


def body(lambdas, charge_a, charge_b, perturbed, grid_index, spline_weights, spline_slopes):
    atoms_here = charge_a.shape[1]
    slab_count = lax.axis_size("slab")
    slab_depth = NZ // slab_count
    flag_values = perturbed.astype(jnp.float32)
    charges = charge_a + flag_values * lambdas[:, None] * (charge_b - charge_a)
    charge_steps = flag_values * (charge_b - charge_a)
    weight_windows = jnp.moveaxis(spline_weights, 2, 0)
    slope_windows = jnp.moveaxis(spline_slopes, 2, 0)
    index_windows = jnp.moveaxis(grid_index, 1, 0)
    cosine_x, sine_x = dft_tables(NX)
    cosine_y, sine_y = dft_tables(NY)
    cosine_z, sine_z = dft_tables(NZ)
    planar = (cosine_x, sine_x, cosine_y, sine_y)
    plane_count = slab_depth + 3
    column_count = NX // slab_count
    first_plane = lax.axis_index("slab") * slab_depth

    def spread_window(inputs):
        return spread_block(inputs[0], inputs[1], inputs[2], first_plane, plane_count)

    extended = lax.map(spread_window, (charges, index_windows, weight_windows))
    reach_count = (slab_depth + 2) // slab_depth
    owned_grid = extended[:, :slab_depth]
    for distance in range(1, reach_count + 1):
        last_plane = min(plane_count, (distance + 1) * slab_depth)
        arrived = passed_along(extended[:, distance * slab_depth : last_plane], "slab", distance)
        owned_grid = owned_grid + jnp.pad(
            arrived, ((0, 0), (0, slab_depth - arrived.shape[1]), (0, 0), (0, 0))
        )
    slab_spectrum = xy_forward(owned_grid, planar)
    influence = influence_block(lax.axis_index("slab") * column_count, column_count)
    stacked, energy_part = column_transform(
        lax.all_to_all(slab_spectrum, "slab", split_axis=3, concat_axis=2, tiled=True),
        influence,
        cosine_z,
        sine_z,
    )
    slab_values = lax.all_to_all(stacked, "slab", split_axis=2, concat_axis=3, tiled=True)
    slab_values, energy_part = (slab_values, energy_part)
    potential = xy_inverse(slab_values, planar)
    pieces = [potential]
    for distance in range(1, reach_count + 1):
        depth_taken = min(slab_depth, plane_count - distance * slab_depth)
        pieces.append(passed_along(potential[:, :depth_taken], "slab", -distance))
    potential_field = jnp.concatenate(pieces, axis=1)

    def sample_window(inputs):
        charge, charge_step, cell_index, weights, slopes, values = inputs
        return sample_block(
            charge, charge_step, cell_index, weights, slopes, values, first_plane, plane_count
        )

    window_forces, derivative_part = lax.map(
        sample_window,
        (charges, charge_steps, index_windows, weight_windows, slope_windows, potential_field),
    )
    forces = jnp.moveaxis(window_forces, 0, 1)
    energy_total = lax.psum(energy_part, "slab")
    derivative_total = lax.psum(derivative_part, "slab")
    atom_total = atoms_here * slab_count
    return (forces, energy_total / atom_total, derivative_total / atom_total)


def solution(mesh):
    return jax.shard_map(
        body,
        mesh=mesh,
        in_specs=(
            P("win"),
            P("win", "slab"),
            P("win", "slab"),
            P("win", "slab"),
            P(None, "win", "slab"),
            P(None, None, "win", "slab"),
            P(None, None, "win", "slab"),
        ),
        out_specs=(P(None, "win", "slab"), P("win"), P("win")),
        check_vma=False,
    )
```

profile of v0, /device:TPU:0, one launch (start us, length us, event | category | flops | bytes accessed | tf_op | source)
XLA Modules:
  0.0 637.9 jit_solution(1168671799262427273)
XLA Ops:
  3.1 25.3 %while.26 = (s32[]{:T(128)}, f32[4,19,128,128]{2,3,1,0:T(8,128)}, s32[4,3,512]{2,1,0:T(4,128)S(1)}, s32[]{:T(128)}, f32[4,3,4,512]{3,2,1,0:T(4,128)S(1)}, /*inde...) while((s32[]{:T(128)}, f32[4,19,128,128]{2,3,1,0:T(8,128)}, ...), condition=%wide.region_1.2_spmd, body=%wide.region_0.1_spmd.sunk | while | flops 1915456512 | bytes 2517685 | solution.py:167
  4.1 5.4 fusion.314
  10.4 5.4 fusion.314
  16.7 5.4 fusion.314
  23.0 5.4 fusion.314
  30.7 12.5 %collective-permute-done = f32[4,3,128,128]{2,3,1,0:T(8,128)S(1)} collective-permute-done((f32[4,3,128,128]{2,3,1,0:T(8,128)S(1)}, f32[4,3,128,128]{2,3,1,0:T(8,128)S(1)}, u32[]{:S(2)}, u32[]{:S(2)}) %collective-permute-start) | collective-permute-done | bytes 786464 | tf_op jit(solution)/shard_map/ppermute | solution.py:17
  43.2 6.1 fusion.130
  49.3 6.9 %fusion.110 = f32[4,16,128,128]{3,2,1,0:T(8,128)S(1)} fusion(f32[4,16,128,128]{3,2,1,0:T(8,128)S(1)} %fusion.130), kind=kOutput, calls=%fused_computation.250 | convolution fusion | flops 1611890688 | bytes 8388608 | tf_op jit(solution)/shard_map/wpkb,bl->wpkl/dot_general | solution.py:85
  56.2 7.4 %fusion.108 = f32[4,16,128,128]{3,2,1,0:T(8,128)S(1)} fusion(f32[4,16,128,128]{3,2,1,0:T(8,128)S(1)} %fusion.130), kind=kOutput, calls=%fused_computation.248 | convolution fusion | flops 1611890688 | bytes 8388608 | tf_op jit(solution)/shard_map/wpkb,bl->wpkl/dot_general | solution.py:88
  67.6 7.5 %add_bitcast_fusion.3 = f32[4,1,16,128,128]{4,3,2,0,1:T(8,128)S(1)} fusion(f32[4,16,128,128]{3,2,1,0:T(8,128)S(1)} %fusion.110, f32[4,16,128,128]{3,2,1,0:T(8,128)S(1)} %fusion.131), kind=kOutput, calls=%fused_computation.264 | convolution fusion | flops 1611890688 | bytes 12582912 | tf_op jit(solution)/shard_map/wpkb,bl->wpkl/dot_general | solution.py:85
  75.1 7.1 %subtract_bitcast_fusion.2 = f32[4,1,16,128,128]{4,3,2,0,1:T(8,128)S(1)} fusion(f32[4,16,128,128]{3,2,1,0:T(8,128)S(1)} %fusion.108, f32[4,16,128,128]{3,2,1,0:T(8,128)S(1)} %fusion.131), kind=kOutput, calls=%fused_computation.263 | convolution fusion | flops 1611890688 | bytes 12582912 | tf_op jit(solution)/shard_map/wpkb,bl->wpkl/dot_general | solution.py:90
  83.3 8.1 %copy.64 = f32[4,2,16,128,128]{4,2,0,1,3:T(8,128)} copy(f32[4,2,16,128,128]{4,3,2,0,1:T(8,128)S(1)} %pad_maximum_fusion) | data formatting | bytes 16777216 | tf_op jit(solution)/shard_map/stack | solution.py:91
  91.4 5.1 all-to-all-start
  97.1 93.5 %all-to-all-done = f32[4,2,16,128,128]{4,2,0,1,3:T(8,128)} async-done(((f32[4,2,16,128,128]{4,2,0,1,3:T(8,128)}), f32[4,2,16,128,128]{4,2,0,1,3:T(8,128)}, u32[]{:S(2)}, u32[]{:S(2)}) %all-to-all-start) | async-done | bytes 8388640 | tf_op jit(solution)/shard_map/all_to_all | solution.py:179
  190.6 8.2 %copy.66 = f32[4,2,8,16,16,128]{5,4,3,2,1,0:T(8,128)S(1)} copy(f32[4,2,8,16,16,128]{5,3,0,1,4,2:T(8,128)} %bitcast.86) | data formatting | bytes 16777216 | tf_op jit(solution)/shard_map/all_to_all | solution.py:179
  202.6 5.3 copy.119
  208.0 7.3 %fusion.102 = f32[4,16,128,128]{3,2,1,0:T(8,128)} fusion(f32[4,1,128,16,128]{2,4,3,0,1:T(8,128)} %copy.119), kind=kOutput, calls=%fused_computation.242 | convolution fusion | flops 1610842112 | bytes 8388608 | tf_op jit(solution)/shard_map/kz,nzab->nkab/dot_general | solution.py:126
  215.3 5.5 fusion.100
  220.8 5.3 copy.118
  226.1 6.7 %fusion.136 = f32[4,16,128,128]{3,2,1,0:T(8,128)S(1)} fusion(f32[4,16,128,128]{3,2,1,0:T(8,128)} %fusion.102, f32[4,1,128,16,128]{2,4,3,0,1:T(8,128)} %copy.118), kind=kOutput, calls=%fused_computation.278 | convolution fusion | flops 1611890688 | bytes 12582912 | tf_op jit(solution)/shard_map/kz,nzab->nkab/dot_general | solution.py:126
  257.7 10.3 %copy.69 = f32[4,2,128,16,128]{4,3,0,1,2:T(8,128)} copy(f32[4,2,128,16,128]{2,4,3,0,1:T(8,128)} %pad_maximum_fusion.1) | data formatting | bytes 16777216 | tf_op jit(solution)/shard_map/stack | solution.py:143
  267.9 97.8 %all_to_all.36 = f32[4,2,128,16,128]{4,3,0,1,2:T(8,128)S(1)} all-to-all(f32[4,2,128,16,128]{4,3,0,1,2:T(8,128)} %copy.69), channel_id=1, replica_groups=mesh['win'=4,'slab'=8] {'slab'}, dimensions={2} | all-to-all | bytes 16777216 | tf_op jit(solution)/shard_map/all_to_all | solution.py:184
  382.7 7.2 %fusion.116 = f32[4,16,128,128]{3,2,1,0:T(8,128)S(1)} fusion(f32[4,16,128,128]{3,2,1,0:T(8,128)S(1)} %fusion.126, f32[4,16,128,128]{3,2,1,0:T(8,128)S(1)} %fusion.124), kind=kOutput, calls=%fused_computation.257 | convolution fusion | flops 1611890688 | bytes 12582912 | tf_op jit(solution)/shard_map/ak,wpkb->wpab/dot_general | solution.py:104
  389.9 7.0 %subtract_bitcast_fusion = f32[4,16,128,128]{2,3,1,0:T(8,128)S(1)} fusion(f32[4,16,128,128]{3,2,1,0:T(8,128)S(1)} %fusion.116, f32[4,16,128,128]{3,2,1,0:T(8,128)S(1)} %fusion.125, f32[4,16,128,128]{3,2,1,0:T(8,128)S(1)} %fusion.127), kind=kOutput, calls=%fused_computation.256 | convolution fusion | flops 1612939264 | bytes 16777216 | tf_op jit(solution)/shard_map/ak,wpkb->wpab/dot_general | solution.py:104
  399.1 9.4 %collective-permute-done.1 = f32[4,3,128,128]{2,3,1,0:T(8,128)S(1)} collective-permute-done((f32[4,3,128,128]{2,3,1,0:T(8,128)S(1)}, f32[4,3,128,128]{2,3,1,0:T(8,128)S(1)}, u32[]{:S(2)}, u32[]{:S(2)}) %collective-permute-start.1) | collective-permute-done | bytes 786464 | tf_op jit(solution)/shard_map/ppermute | solution.py:17
  408.5 5.0 pad_maximum_fusion.2
  413.5 209.0 %while.27 = (s32[]{:T(128)}, f32[4,3,512]{2,0,1:T(4,128)S(1)}, f32[4]{0:T(128)S(1)}, f32[4,512]{1,0:T(4,128)}, s32[4,3,512]{2,1,0:T(4,128)S(1)}, /*index=5*/s32[...) while((s32[]{:T(128)}, f32[4,3,512]{2,0,1:T(4,128)S(1)}, ...), condition=%wide.region_4.5_spmd, body=%wide.region_2.4_spmd.sunk | while | flops 3872960512 | bytes 29543656 | solution.py:199
  413.8 5.9 fusion.327
  420.7 11.9 %fusion.328 = f32[512,1,19]{2,1,0:T(1,128)S(1)} fusion(f32[512,128,1]{1,2,0:T(1,128)S(1)} %bitcast.372, f32[512,19,128]{2,0,1:T(8,128)S(1)} %fusion.327), kind=kOutput, calls=%fused_computation.94.clone.1 | convolution fusion | flops 14942208 | bytes 5281792 | tf_op jit(solution)/shard_map/while/body/eval_jaxpr/ia,ipa->ip/dot_general | solution.py:73
  432.6 5.9 fusion.325
  438.5 12.1 %fusion.329 = f32[512,1,19]{2,1,0:T(1,128)S(1)} fusion(f32[512,128,1]{1,2,0:T(1,128)S(1)} %bitcast.379, f32[512,19,128]{2,0,1:T(8,128)S(1)} %fusion.325), kind=kOutput, calls=%fused_computation.92.clone.1 | convolution fusion | flops 14942208 | bytes 5281792 | tf_op jit(solution)/shard_map/while/body/eval_jaxpr/ia,ipa->ip/dot_general | solution.py:71
  450.6 11.9 %fusion.326 = f32[512,1,19]{2,1,0:T(1,128)S(1)} fusion(f32[512,128,1]{1,2,0:T(1,128)S(1)} %bitcast.373, f32[512,19,128]{2,0,1:T(8,128)S(1)} %fusion.325), kind=kOutput, calls=%fused_computation.90.clone.1 | convolution fusion | flops 14942208 | bytes 5281792 | tf_op jit(solution)/shard_map/while/body/eval_jaxpr/ia,ipa->ip/dot_general | solution.py:70
  465.8 5.9 fusion.327
  472.6 12.1 %fusion.328 = f32[512,1,19]{2,1,0:T(1,128)S(1)} fusion(f32[512,128,1]{1,2,0:T(1,128)S(1)} %bitcast.372, f32[512,19,128]{2,0,1:T(8,128)S(1)} %fusion.327), kind=kOutput, calls=%fused_computation.94.clone.1 | convolution fusion | flops 14942208 | bytes 5281792 | tf_op jit(solution)/shard_map/while/body/eval_jaxpr/ia,ipa->ip/dot_general | solution.py:73
  484.7 5.9 fusion.325
  490.7 11.9 %fusion.329 = f32[512,1,19]{2,1,0:T(1,128)S(1)} fusion(f32[512,128,1]{1,2,0:T(1,128)S(1)} %bitcast.379, f32[512,19,128]{2,0,1:T(8,128)S(1)} %fusion.325), kind=kOutput, calls=%fused_computation.92.clone.1 | convolution fusion | flops 14942208 | bytes 5281792 | tf_op jit(solution)/shard_map/while/body/eval_jaxpr/ia,ipa->ip/dot_general | solution.py:71
  502.5 11.9 %fusion.326 = f32[512,1,19]{2,1,0:T(1,128)S(1)} fusion(f32[512,128,1]{1,2,0:T(1,128)S(1)} %bitcast.373, f32[512,19,128]{2,0,1:T(8,128)S(1)} %fusion.325), kind=kOutput, calls=%fused_computation.90.clone.1 | convolution fusion | flops 14942208 | bytes 5281792 | tf_op jit(solution)/shard_map/while/body/eval_jaxpr/ia,ipa->ip/dot_general | solution.py:70
  517.9 5.9 fusion.327
  524.7 11.9 %fusion.328 = f32[512,1,19]{2,1,0:T(1,128)S(1)} fusion(f32[512,128,1]{1,2,0:T(1,128)S(1)} %bitcast.372, f32[512,19,128]{2,0,1:T(8,128)S(1)} %fusion.327), kind=kOutput, calls=%fused_computation.94.clone.1 | convolution fusion | flops 14942208 | bytes 5281792 | tf_op jit(solution)/shard_map/while/body/eval_jaxpr/ia,ipa->ip/dot_general | solution.py:73
  536.6 5.9 fusion.325
  542.6 11.9 %fusion.329 = f32[512,1,19]{2,1,0:T(1,128)S(1)} fusion(f32[512,128,1]{1,2,0:T(1,128)S(1)} %bitcast.379, f32[512,19,128]{2,0,1:T(8,128)S(1)} %fusion.325), kind=kOutput, calls=%fused_computation.92.clone.1 | convolution fusion | flops 14942208 | bytes 5281792 | tf_op jit(solution)/shard_map/while/body/eval_jaxpr/ia,ipa->ip/dot_general | solution.py:71
  554.5 12.1 %fusion.326 = f32[512,1,19]{2,1,0:T(1,128)S(1)} fusion(f32[512,128,1]{1,2,0:T(1,128)S(1)} %bitcast.373, f32[512,19,128]{2,0,1:T(8,128)S(1)} %fusion.325), kind=kOutput, calls=%fused_computation.90.clone.1 | convolution fusion | flops 14942208 | bytes 5281792 | tf_op jit(solution)/shard_map/while/body/eval_jaxpr/ia,ipa->ip/dot_general | solution.py:70
  569.8 5.9 fusion.327
  576.6 11.9 %fusion.328 = f32[512,1,19]{2,1,0:T(1,128)S(1)} fusion(f32[512,128,1]{1,2,0:T(1,128)S(1)} %bitcast.372, f32[512,19,128]{2,0,1:T(8,128)S(1)} %fusion.327), kind=kOutput, calls=%fused_computation.94.clone.1 | convolution fusion | flops 14942208 | bytes 5281792 | tf_op jit(solution)/shard_map/while/body/eval_jaxpr/ia,ipa->ip/dot_general | solution.py:73
  588.5 5.9 fusion.325
  594.5 12.1 %fusion.329 = f32[512,1,19]{2,1,0:T(1,128)S(1)} fusion(f32[512,128,1]{1,2,0:T(1,128)S(1)} %bitcast.379, f32[512,19,128]{2,0,1:T(8,128)S(1)} %fusion.325), kind=kOutput, calls=%fused_computation.92.clone.1 | convolution fusion | flops 14942208 | bytes 5281792 | tf_op jit(solution)/shard_map/while/body/eval_jaxpr/ia,ipa->ip/dot_general | solution.py:71
  606.6 11.9 %fusion.326 = f32[512,1,19]{2,1,0:T(1,128)S(1)} fusion(f32[512,128,1]{1,2,0:T(1,128)S(1)} %bitcast.373, f32[512,19,128]{2,0,1:T(8,128)S(1)} %fusion.325), kind=kOutput, calls=%fused_computation.90.clone.1 | convolution fusion | flops 14942208 | bytes 5281792 | tf_op jit(solution)/shard_map/while/body/eval_jaxpr/ia,ipa->ip/dot_general | solution.py:70
  622.5 14.6 %all-reduce.1 = (f32[4]{0:T(128)S(1)}, f32[4]{0:T(128)S(1)}) all-reduce(f32[4]{0:T(128)S(1)} %broadcast_multiply_fusion.2, f32[4]{0:T(128)S(1)} %get-tuple-element.210), channel_id=1, replica_groups=mesh['win'=4,'slab'=8] {'slab'}, use_global_device_ids=true, to_apply=%region_6.7 | all-reduce | flops 8 | bytes 64 | tf_op jit(solution)/shard_map/psum | solution.py:204
  (146 shorter events, 77.3 us)
Async XLA Ops:
  28.4 20.9 %copy-start.4 = (f32[4,512]{1,0:T(4,128)}, f32[4,512]{1,0:T(4,128)S(1)}, u32[]{:S(2)}) copy-start(f32[4,512]{1,0:T(4,128)S(1)} %get-tuple-element.728) | copy-start | bytes 24580
  29.6 13.6 %collective-permute-start = (f32[4,3,128,128]{2,3,1,0:T(8,128)S(1)}, f32[4,3,128,128]{2,3,1,0:T(8,128)S(1)}, u32[]{:S(2)}, u32[]{:S(2)}) collective-permute-start(f32[4,3,128,128]{2,3,1,0:T(8,128)S(1)} %slice.373), channel_id=1, source_target_pairs={{0,1},{1,2},{2,3},{3,4},{4,5},{5,6},{6,7},{7,0},{8,9},{9,10},{10,1... | collective-permute-start | bytes 2359304 | tf_op jit(solution)/shard_map/ppermute | solution.py:17
  49.3 14.4 %slice-start = ((s8[4980736]{0:T(1024)(128)(4,1)}), s8[4194304]{0:T(1024)(128)(4,1)S(1)}, s32[]{:S(2)}) async-start(s8[4980736]{0:T(1024)(128)(4,1)} %bitcast.380), calls=%async_computation.2 | async-start | bytes 8388608
  56.2 7.5 %slice-start.1 = ((s8[4980736]{0:T(1024)(128)(4,1)}), s8[786432]{0:T(1024)(128)(4,1)S(1)}, s32[]{:S(2)}) async-start(s8[4980736]{0:T(1024)(128)(4,1)} %bitcast.380), calls=%async_computation.3 | async-start | bytes 1572864
  91.4 99.2 %all-to-all-start = ((f32[4,2,16,128,128]{4,2,0,1,3:T(8,128)}), f32[4,2,16,128,128]{4,2,0,1,3:T(8,128)}, u32[]{:S(2)}, u32[]{:S(2)}) async-start(f32[4,2,16,128,128]{4,2,0,1,3:T(8,128)} %copy.64), calls=%async_computation | async-start | bytes 16777216 | tf_op jit(solution)/shard_map/all_to_all | solution.py:179
  208.0 7.3 %copy-start.1 = (f32[4,1,128,16,128]{2,4,3,0,1:T(8,128)S(1)}, f32[4,1,128,16,128]{2,4,3,0,1:T(8,128)}, u32[]{:S(2)}) copy-start(f32[4,1,128,16,128]{2,4,3,0,1:T(8,128)} %copy.119) | copy-start | bytes 12582916
  236.8 4.0 copy-start
  236.8 4.0 copy-start.3
  389.9 9.2 %copy-start.5 = (f32[3,4,4,512]{3,2,1,0:T(4,128)S(1)}, f32[3,4,4,512]{3,2,1,0:T(4,128)}, u32[]{:S(2)}) copy-start(f32[3,4,4,512]{3,2,1,0:T(4,128)} %param.17) | copy-start | bytes 294916
  396.9 2.0 copy-start.2
  399.0 9.6 %collective-permute-start.1 = (f32[4,3,128,128]{2,3,1,0:T(8,128)S(1)}, f32[4,3,128,128]{2,3,1,0:T(8,128)S(1)}, u32[]{:S(2)}, u32[]{:S(2)}) collective-permute-start(f32[4,3,128,128]{2,3,1,0:T(8,128)S(1)} %slice.383), channel_id=1, source_target_pairs={{0,7},{1,0},{2,1},{3,2},{4,3},{5,4},{6,5},{7,6},{8,15},{9,8},{10,9... | collective-permute-start | bytes 2359304 | tf_op jit(solution)/shard_map/ppermute | solution.py:17
  622.5 15.1 %copy-start.6 = (f32[4,3,512]{2,0,1:T(4,128)}, f32[4,3,512]{2,0,1:T(4,128)S(1)}, u32[]{:S(2)}) copy-start(f32[4,3,512]{2,0,1:T(4,128)S(1)} %get-tuple-element.209) | copy-start | bytes 73732
where the time goes:
time: 644 us; the launch traced here: 638 us
  matrix products  322 us (50%)
  waiting for transfers between devices  115 us (18%)
  blocking collectives  112 us (17%)
  local copies, waits for them, and re-layouts  52.8 us (8%)
  other arithmetic  25.1 us (4%)
    all_to_all x1, blocking collectives, body(): lax.all_to_all(stacked, 'slab', split_axis=2, concat_axis=3, tiled=True)  97.8 us
    all_to_all x1, waiting for transfers between devices, body(): lax.all_to_all(slab_spectrum, 'slab', split_axis=3, concat_axis=2, tiled=...  93.5 us
    dot_general x4, matrix products, sample_block(): jnp.einsum('ia,ipa->ip', steep_x, along_rows, precision=highest)  48 us
    dot_general x4, matrix products, sample_block(): jnp.einsum('ia,ipa->ip', rows_x, along_steep, precision=highest)  47.8 us
    dot_general x4, matrix products, sample_block(): reduced = jnp.einsum('ia,ipa->ip', rows_x, along_rows, precision=highest)  47.8 us
    dot_general x4, matrix products, sample_block(): along_steep = jnp.einsum('pab,ib->ipa', values, steep_y, precision=highest)  23.8 us
    dot_general x4, matrix products, sample_block(): along_rows = jnp.einsum('pab,ib->ipa', values, rows_y, precision=highest)  23.8 us
    ppermute x2, waiting for transfers between devices, passed_along(): return lax.ppermute(value, axis, pairs)  22 us
  transfers between devices with their start and end apart: 3, of which 3 were waited for; matrix products, arithmetic and copies ran while one was open for 0% of the time, Pallas kernels for 0%

commit v1 on v0

--- a/solution.py
+++ b/solution.py
@@ -9,6 +9,22 @@
 NZ = 128
 highest = lax.Precision.HIGHEST
 gauss_width = 2.0
+
+
+def pairwise_exchange(value, axis, split, join):
+    ways, here = (lax.axis_size(axis), lax.axis_index(axis))
+    width = value.shape[split] // ways
+    dims = list(value.shape)
+    dims[split] = width
+    height = dims[join]
+    dims[join] = height * ways
+    full = jnp.zeros(dims, value.dtype)
+    for mask in range(ways):
+        part = lax.dynamic_slice_in_dim(value, (here ^ mask) * width, width, axis=split)
+        if mask:
+            part = lax.ppermute(part, axis, [(d, d ^ mask) for d in range(ways)])
+        full = lax.dynamic_update_slice_in_dim(full, part, (here ^ mask) * height, axis=join)
+    return full
 
 
 def passed_along(value, axis, steps):
@@ -176,10 +192,7 @@
     slab_spectrum = xy_forward(owned_grid, planar)
     influence = influence_block(lax.axis_index("slab") * column_count, column_count)
     stacked, energy_part = column_transform(
-        lax.all_to_all(slab_spectrum, "slab", split_axis=3, concat_axis=2, tiled=True),
-        influence,
-        cosine_z,
-        sine_z,
+        pairwise_exchange(slab_spectrum, "slab", 3, 2), influence, cosine_z, sine_z
     )
     slab_values = lax.all_to_all(stacked, "slab", split_axis=2, concat_axis=3, tiled=True)
     slab_values, energy_part = (slab_values, energy_part)

time: 644 us -> 1010 us (1.57)
  local copies, waits for them, and re-layouts: 52.8 us -> 480 us
  waiting for transfers between devices: 115 us -> 39.4 us
    dynamic_update_slice x0 -> x8, local copies, waits for them, and re-layouts: none -> 404 us  [pairwise_exchange(): lax.dynamic_update_slice_in_dim(full, part, (here ^ mask) * height, axis=...]
    all_to_all x1 -> x0, waiting for transfers between devices: 93.5 us -> none  [body(): lax.all_to_all(slab_spectrum, 'slab', split_axis=3, concat_axis=2, tiled=...]
    ppermute x0 -> x7, local copies, waits for them, and re-layouts: none -> 39.2 us  [pairwise_exchange(): part = lax.ppermute(part, axis, [(d, d ^ mask) for d in range(ways)])]
    ppermute x0 -> x7, waiting for transfers between devices: none -> 17.4 us  [pairwise_exchange(): part = lax.ppermute(part, axis, [(d, d ^ mask) for d in range(ways)])]
  transfers between devices with their start and end apart: 3 -> 9, of which waited for: 3 -> 3; matrix products, arithmetic and copies ran while one was open for 0% -> 40% of each run, Pallas kernels for 0% -> 0%
where the time goes in v1:
time: 1010 us; the launch traced here: 995 us
  local copies, waits for them, and re-layouts  480 us (48%)
  matrix products  317 us (31%)
  blocking collectives  112 us (11%)
  waiting for transfers between devices  39.4 us (4%)
  other arithmetic  34 us (3%)
    dynamic_update_slice x8, local copies, waits for them, and re-layouts, pairwise_exchange(): lax.dynamic_update_slice_in_dim(full, part, (here ^ mask) * height, axis=...  404 us
    all_to_all x1, blocking collectives, body(): lax.all_to_all(stacked, 'slab', split_axis=2, concat_axis=3, tiled=True)  97.8 us
    dot_general x4, matrix products, sample_block(): jnp.einsum('ia,ipa->ip', steep_x, along_rows, precision=highest)  48 us
    dot_general x4, matrix products, sample_block(): jnp.einsum('ia,ipa->ip', rows_x, along_steep, precision=highest)  47.8 us
    dot_general x4, matrix products, sample_block(): reduced = jnp.einsum('ia,ipa->ip', rows_x, along_rows, precision=highest)  47.8 us
    ppermute x7, local copies, waits for them, and re-layouts, pairwise_exchange(): part = lax.ppermute(part, axis, [(d, d ^ mask) for d in range(ways)])  39.2 us
    dot_general x4, matrix products, sample_block(): along_steep = jnp.einsum('pab,ib->ipa', values, steep_y, precision=highest)  23.8 us
    dot_general x4, matrix products, sample_block(): along_rows = jnp.einsum('pab,ib->ipa', values, rows_y, precision=highest)  23.8 us
  transfers between devices with their start and end apart: 9, of which 3 were waited for; matrix products, arithmetic and copies ran while one was open for 40% of the time, Pallas kernels for 0%

profile of v1, /device:TPU:0, one launch (start us, length us, event | category | flops | bytes accessed | tf_op | source)
XLA Modules:
  0.0 994.8 jit_solution(9527563143507040582)
XLA Ops:
  3.7 25.2 %while.26 = (s32[]{:T(128)}, f32[4,19,128,128]{2,3,1,0:T(8,128)}, s32[4,3,512]{2,1,0:T(4,128)S(1)}, s32[]{:T(128)}, f32[4,3,4,512]{3,2,1,0:T(4,128)S(1)}, /*inde...) while((s32[]{:T(128)}, f32[4,19,128,128]{2,3,1,0:T(8,128)}, ...), condition=%wide.region_1.2_spmd, body=%wide.region_0.1_spmd.sunk | while | flops 1915456512 | bytes 2517685 | solution.py:183
  31.8 12.5 %collective-permute-done = f32[4,3,128,128]{2,3,1,0:T(8,128)S(1)} collective-permute-done((f32[4,3,128,128]{2,3,1,0:T(8,128)S(1)}, f32[4,3,128,128]{2,3,1,0:T(8,128)S(1)}, u32[]{:S(2)}, u32[]{:S(2)}) %collective-permute-start) | collective-permute-done | bytes 786464 | tf_op jit(solution)/shard_map/ppermute | solution.py:33
  44.4 6.1 fusion.126
  50.4 6.9 fusion.100
  57.4 7.2 fusion.102
  68.5 7.4 subtract_bitcast_fusion.2
  75.9 7.6 add_bitcast_fusion.3
  96.0 17.4 %collective-permute-done.2 = f32[4,2,16,16,128]{4,3,2,0,1:T(8,128)S(1)} collective-permute-done((f32[4,2,16,16,128]{4,3,2,0,1:T(8,128)}, f32[4,2,16,16,128]{4,3,2,0,1:T(8,128)S(1)}, u32[]{:S(2)}, u32[]{:S(2)}) %collective-permute-start.2) | collective-permute-done | bytes 1048608 | tf_op jit(solution)/shard_map/ppermute | solution.py:25
  124.0 39.3 %dynamic_update_slice.45 = f32[4,2,128,16,128]{2,4,3,0,1:T(8,128)} dynamic-update-slice(f32[4,2,128,16,128]{2,4,3,0,1:T(8,128)} %broadcast_in_dim.30, f32[4,2,16,16,128]{2,4,3,0,1:T(8,128)} %copy.56, s32[]{:T(128)} %constant.329.clone.1, s32[]{:T(128)} %constant.329.clone.1, s32[]{:T(128)S(6)} %select_n.322, s32[]{:T(128)} %constant.329.clone.1, s32[]{:T(128)} %constant.329.clone.1) | dynamic-update-slice | bytes 2097156 | tf_op jit(solution)/shard_map/dynamic_update_slice | solution.py:26
  167.9 52.2 %dynamic_update_slice.46 = f32[4,2,128,16,128]{2,4,3,0,1:T(8,128)} dynamic-update-slice(f32[4,2,128,16,128]{2,4,3,0,1:T(8,128)} %dynamic_update_slice.45, f32[4,2,16,16,128]{2,4,3,0,1:T(8,128)} %copy.57, s32[]{:T(128)} %constant.329.clone.1, s32[]{:T(128)} %constant.329.clone.1, s32[]{:T(128)S(6)} %select_n.323, s32[]{:T(128)} %constant.329.clone.1, s32[]{:T(128)} %constant.329.clone.1) | dynamic-update-slice | bytes 2097156 | tf_op jit(solution)/shard_map/dynamic_update_slice | solution.py:26
  224.7 52.2 %dynamic_update_slice.47 = f32[4,2,128,16,128]{2,4,3,0,1:T(8,128)} dynamic-update-slice(f32[4,2,128,16,128]{2,4,3,0,1:T(8,128)} %dynamic_update_slice.46, f32[4,2,16,16,128]{2,4,3,0,1:T(8,128)} %copy.58, s32[]{:T(128)} %constant.329.clone.1, s32[]{:T(128)} %constant.329.clone.1, s32[]{:T(128)S(6)} %select_n.324, s32[]{:T(128)} %constant.329.clone.1, s32[]{:T(128)} %constant.329.clone.1) | dynamic-update-slice | bytes 2097156 | tf_op jit(solution)/shard_map/dynamic_update_slice | solution.py:26
  276.9 6.0 copy.59
  282.9 52.2 %dynamic_update_slice.48 = f32[4,2,128,16,128]{2,4,3,0,1:T(8,128)} dynamic-update-slice(f32[4,2,128,16,128]{2,4,3,0,1:T(8,128)} %dynamic_update_slice.47, f32[4,2,16,16,128]{2,4,3,0,1:T(8,128)} %copy.59, s32[]{:T(128)} %constant.329.clone.1, s32[]{:T(128)} %constant.329.clone.1, s32[]{:T(128)S(6)} %select_n.325, s32[]{:T(128)} %constant.329.clone.1, s32[]{:T(128)} %constant.329.clone.1) | dynamic-update-slice | bytes 2097156 | tf_op jit(solution)/shard_map/dynamic_update_slice | solution.py:26
  335.0 6.0 copy.60
  341.0 52.2 %dynamic_update_slice.49 = f32[4,2,128,16,128]{2,4,3,0,1:T(8,128)} dynamic-update-slice(f32[4,2,128,16,128]{2,4,3,0,1:T(8,128)} %dynamic_update_slice.48, f32[4,2,16,16,128]{2,4,3,0,1:T(8,128)} %copy.60, s32[]{:T(128)} %constant.329.clone.1, s32[]{:T(128)} %constant.329.clone.1, s32[]{:T(128)S(6)} %select_n.326, s32[]{:T(128)} %constant.329.clone.1, s32[]{:T(128)} %constant.329.clone.1) | dynamic-update-slice | bytes 2097156 | tf_op jit(solution)/shard_map/dynamic_update_slice | solution.py:26
  393.2 6.0 copy.61
  399.2 52.2 %dynamic_update_slice.50 = f32[4,2,128,16,128]{2,4,3,0,1:T(8,128)} dynamic-update-slice(f32[4,2,128,16,128]{2,4,3,0,1:T(8,128)} %dynamic_update_slice.49, f32[4,2,16,16,128]{2,4,3,0,1:T(8,128)} %copy.61, s32[]{:T(128)} %constant.329.clone.1, s32[]{:T(128)} %constant.329.clone.1, s32[]{:T(128)S(6)} %select_n.327, s32[]{:T(128)} %constant.329.clone.1, s32[]{:T(128)} %constant.329.clone.1) | dynamic-update-slice | bytes 2097156 | tf_op jit(solution)/shard_map/dynamic_update_slice | solution.py:26
  451.3 6.0 copy.62
  457.3 52.2 %dynamic_update_slice.51 = f32[4,2,128,16,128]{2,4,3,0,1:T(8,128)} dynamic-update-slice(f32[4,2,128,16,128]{2,4,3,0,1:T(8,128)} %dynamic_update_slice.50, f32[4,2,16,16,128]{2,4,3,0,1:T(8,128)} %copy.62, s32[]{:T(128)} %constant.329.clone.1, s32[]{:T(128)} %constant.329.clone.1, s32[]{:T(128)S(6)} %select_n.328, s32[]{:T(128)} %constant.329.clone.1, s32[]{:T(128)} %constant.329.clone.1) | dynamic-update-slice | bytes 2097156 | tf_op jit(solution)/shard_map/dynamic_update_slice | solution.py:26
  509.5 6.0 copy.63
  515.5 52.2 %dynamic_update_slice.52 = f32[4,2,128,16,128]{2,4,3,0,1:T(8,128)} dynamic-update-slice(f32[4,2,128,16,128]{2,4,3,0,1:T(8,128)} %dynamic_update_slice.51, f32[4,2,16,16,128]{2,4,3,0,1:T(8,128)} %copy.63, s32[]{:T(128)} %constant.329.clone.1, s32[]{:T(128)} %constant.329.clone.1, s32[]{:T(128)S(6)} %select_n.329, s32[]{:T(128)} %constant.329.clone.1, s32[]{:T(128)} %constant.329.clone.1) | dynamic-update-slice | bytes 2097156 | tf_op jit(solution)/shard_map/dynamic_update_slice | solution.py:26
  567.6 6.2 fusion.119
  606.6 10.3 %copy.64 = f32[4,2,128,16,128]{4,3,0,1,2:T(8,128)} copy(f32[4,2,128,16,128]{2,4,3,0,1:T(8,128)} %pad_maximum_fusion) | data formatting | bytes 16777216 | tf_op jit(solution)/shard_map/stack | solution.py:159
  616.9 97.8 %all_to_all.18 = f32[4,2,128,16,128]{4,3,0,1,2:T(8,128)S(1)} all-to-all(f32[4,2,128,16,128]{4,3,0,1,2:T(8,128)} %copy.64), channel_id=1, replica_groups=mesh['win'=4,'slab'=8] {'slab'}, dimensions={2} | all-to-all | bytes 16777216 | tf_op jit(solution)/shard_map/all_to_all | solution.py:197
  731.7 7.2 fusion.108
  738.9 7.0 subtract_bitcast_fusion
  748.5 9.4 collective-permute-done.8
  762.9 216.4 %while.27 = (s32[]{:T(128)}, f32[4,3,512]{2,0,1:T(4,128)S(1)}, f32[4]{0:T(128)S(1)}, f32[4,512]{1,0:T(4,128)}, s32[4,3,512]{2,1,0:T(4,128)}, /*index=5*/s32[]{:T...) while((s32[]{:T(128)}, f32[4,3,512]{2,0,1:T(4,128)S(1)}, ...), condition=%wide.region_4.5_spmd, body=%wide.region_2.4_spmd.sunk | while | flops 3872960512 | bytes 29543656 | solution.py:212
  765.0 5.9 fusion.326
  771.8 11.9 %fusion.327 = f32[512,1,19]{2,1,0:T(1,128)S(1)} fusion(f32[512,128,1]{1,2,0:T(1,128)S(1)} %bitcast.366, f32[512,19,128]{2,0,1:T(8,128)S(1)} %fusion.326), kind=kOutput, calls=%fused_computation.94.clone.1 | convolution fusion | flops 14942208 | bytes 5281792 | tf_op jit(solution)/shard_map/while/body/eval_jaxpr/ia,ipa->ip/dot_general | solution.py:89
  783.7 5.9 fusion.324
  789.7 12.1 %fusion.328 = f32[512,1,19]{2,1,0:T(1,128)S(1)} fusion(f32[512,128,1]{1,2,0:T(1,128)S(1)} %bitcast.372, f32[512,19,128]{2,0,1:T(8,128)S(1)} %fusion.324), kind=kOutput, calls=%fused_computation.92.clone.1 | convolution fusion | flops 14942208 | bytes 5281792 | tf_op jit(solution)/shard_map/while/body/eval_jaxpr/ia,ipa->ip/dot_general | solution.py:87
  801.8 11.9 %fusion.325 = f32[512,1,19]{2,1,0:T(1,128)S(1)} fusion(f32[512,128,1]{1,2,0:T(1,128)S(1)} %bitcast.367, f32[512,19,128]{2,0,1:T(8,128)S(1)} %fusion.324), kind=kOutput, calls=%fused_computation.90.clone.1 | convolution fusion | flops 14942208 | bytes 5281792 | tf_op jit(solution)/shard_map/while/body/eval_jaxpr/ia,ipa->ip/dot_general | solution.py:86
  818.8 5.9 fusion.326
  825.6 12.1 %fusion.327 = f32[512,1,19]{2,1,0:T(1,128)S(1)} fusion(f32[512,128,1]{1,2,0:T(1,128)S(1)} %bitcast.366, f32[512,19,128]{2,0,1:T(8,128)S(1)} %fusion.326), kind=kOutput, calls=%fused_computation.94.clone.1 | convolution fusion | flops 14942208 | bytes 5281792 | tf_op jit(solution)/shard_map/while/body/eval_jaxpr/ia,ipa->ip/dot_general | solution.py:89
  837.7 5.9 fusion.324
  843.7 11.9 %fusion.328 = f32[512,1,19]{2,1,0:T(1,128)S(1)} fusion(f32[512,128,1]{1,2,0:T(1,128)S(1)} %bitcast.372, f32[512,19,128]{2,0,1:T(8,128)S(1)} %fusion.324), kind=kOutput, calls=%fused_computation.92.clone.1 | convolution fusion | flops 14942208 | bytes 5281792 | tf_op jit(solution)/shard_map/while/body/eval_jaxpr/ia,ipa->ip/dot_general | solution.py:87
  855.5 11.9 %fusion.325 = f32[512,1,19]{2,1,0:T(1,128)S(1)} fusion(f32[512,128,1]{1,2,0:T(1,128)S(1)} %bitcast.367, f32[512,19,128]{2,0,1:T(8,128)S(1)} %fusion.324), kind=kOutput, calls=%fused_computation.90.clone.1 | convolution fusion | flops 14942208 | bytes 5281792 | tf_op jit(solution)/shard_map/while/body/eval_jaxpr/ia,ipa->ip/dot_general | solution.py:86
  872.8 5.9 fusion.326
  879.6 11.9 %fusion.327 = f32[512,1,19]{2,1,0:T(1,128)S(1)} fusion(f32[512,128,1]{1,2,0:T(1,128)S(1)} %bitcast.366, f32[512,19,128]{2,0,1:T(8,128)S(1)} %fusion.326), kind=kOutput, calls=%fused_computation.94.clone.1 | convolution fusion | flops 14942208 | bytes 5281792 | tf_op jit(solution)/shard_map/while/body/eval_jaxpr/ia,ipa->ip/dot_general | solution.py:89
  897.4 11.9 %fusion.328 = f32[512,1,19]{2,1,0:T(1,128)S(1)} fusion(f32[512,128,1]{1,2,0:T(1,128)S(1)} %bitcast.372, f32[512,19,128]{2,0,1:T(8,128)S(1)} %fusion.324), kind=kOutput, calls=%fused_computation.92.clone.1 | convolution fusion | flops 14942208 | bytes 5281792 | tf_op jit(solution)/shard_map/while/body/eval_jaxpr/ia,ipa->ip/dot_general | solution.py:87
  909.3 12.1 %fusion.325 = f32[512,1,19]{2,1,0:T(1,128)S(1)} fusion(f32[512,128,1]{1,2,0:T(1,128)S(1)} %bitcast.367, f32[512,19,128]{2,0,1:T(8,128)S(1)} %fusion.324), kind=kOutput, calls=%fused_computation.90.clone.1 | convolution fusion | flops 14942208 | bytes 5281792 | tf_op jit(solution)/shard_map/while/body/eval_jaxpr/ia,ipa->ip/dot_general | solution.py:86
  926.5 5.9 fusion.326
  933.3 11.9 %fusion.327 = f32[512,1,19]{2,1,0:T(1,128)S(1)} fusion(f32[512,128,1]{1,2,0:T(1,128)S(1)} %bitcast.366, f32[512,19,128]{2,0,1:T(8,128)S(1)} %fusion.326), kind=kOutput, calls=%fused_computation.94.clone.1 | convolution fusion | flops 14942208 | bytes 5281792 | tf_op jit(solution)/shard_map/while/body/eval_jaxpr/ia,ipa->ip/dot_general | solution.py:89
  945.3 5.9 fusion.324
  951.2 12.1 %fusion.328 = f32[512,1,19]{2,1,0:T(1,128)S(1)} fusion(f32[512,128,1]{1,2,0:T(1,128)S(1)} %bitcast.372, f32[512,19,128]{2,0,1:T(8,128)S(1)} %fusion.324), kind=kOutput, calls=%fused_computation.92.clone.1 | convolution fusion | flops 14942208 | bytes 5281792 | tf_op jit(solution)/shard_map/while/body/eval_jaxpr/ia,ipa->ip/dot_general | solution.py:87
  963.3 11.9 %fusion.325 = f32[512,1,19]{2,1,0:T(1,128)S(1)} fusion(f32[512,128,1]{1,2,0:T(1,128)S(1)} %bitcast.367, f32[512,19,128]{2,0,1:T(8,128)S(1)} %fusion.324), kind=kOutput, calls=%fused_computation.90.clone.1 | convolution fusion | flops 14942208 | bytes 5281792 | tf_op jit(solution)/shard_map/while/body/eval_jaxpr/ia,ipa->ip/dot_general | solution.py:86
  979.4 14.6 %all-reduce.1 = (f32[4]{0:T(128)S(1)}, f32[4]{0:T(128)S(1)}) all-reduce(f32[4]{0:T(128)S(1)} %broadcast_multiply_fusion.2, f32[4]{0:T(128)S(1)} %get-tuple-element.210), channel_id=1, replica_groups=mesh['win'=4,'slab'=8] {'slab'}, use_global_device_ids=true, to_apply=%region_6.7 | all-reduce | flops 8 | bytes 64 | tf_op jit(solution)/shard_map/psum | solution.py:217
  (179 shorter events, 153.8 us)
Async XLA Ops:
  28.9 0.6 copy-start.4
  28.9 0.7 copy-start.7
  28.9 0.7 copy-start.8
  30.8 13.6 %collective-permute-start = (f32[4,3,128,128]{2,3,1,0:T(8,128)S(1)}, f32[4,3,128,128]{2,3,1,0:T(8,128)S(1)}, u32[]{:S(2)}, u32[]{:S(2)}) collective-permute-start(f32[4,3,128,128]{2,3,1,0:T(8,128)S(1)} %slice.373), channel_id=1, source_target_pairs={{0,1},{1,2},{2,3},{3,4},{4,5},{5,6},{6,7},{7,0},{8,9},{9,10},{10,1... | collective-permute-start | bytes 2359304 | tf_op jit(solution)/shard_map/ppermute | solution.py:33
  50.4 14.2 %slice-start = ((s8[4980736]{0:T(1024)(128)(4,1)}), s8[4194304]{0:T(1024)(128)(4,1)S(1)}, s32[]{:S(2)}) async-start(s8[4980736]{0:T(1024)(128)(4,1)} %bitcast.373), calls=%async_computation.1 | async-start | bytes 8388608
  57.4 7.3 slice-start.1
  75.9 7.6 copy-start.1
  83.5 3.6 copy-start.2
  87.1 7.2 collective-permute-start.1
  87.1 26.2 %collective-permute-start.2 = (f32[4,2,16,16,128]{4,3,2,0,1:T(8,128)}, f32[4,2,16,16,128]{4,3,2,0,1:T(8,128)S(1)}, u32[]{:S(2)}, u32[]{:S(2)}) collective-permute-start(f32[4,2,16,16,128]{4,3,2,0,1:T(8,128)} %get-tuple-element.375), channel_id=1, source_target_pairs={{0,2},{1,3},{2,0},{3,1},{4,6},{5,7},{6,4},{7,5},{8,10},{9,11},{10,... | collective-permute-start | bytes 3145736 | tf_op jit(solution)/shard_map/ppermute | solution.py:25
  88.4 188.4 %collective-permute-start.3 = (f32[4,2,16,16,128]{4,3,2,0,1:T(8,128)}, f32[4,2,16,16,128]{4,3,2,0,1:T(8,128)}, u32[]{:S(2)}, u32[]{:S(2)}) collective-permute-start(f32[4,2,16,16,128]{4,3,2,0,1:T(8,128)} %get-tuple-element.376), channel_id=1, source_target_pairs={{0,3},{1,2},{2,1},{3,0},{4,7},{5,6},{6,5},{7,4},{8,11},{9,10},{10,... | collective-permute-start | bytes 3145736 | tf_op jit(solution)/shard_map/ppermute | solution.py:25
  88.9 246.1 %collective-permute-start.4 = (f32[4,2,16,16,128]{4,3,2,0,1:T(8,128)}, f32[4,2,16,16,128]{4,3,2,0,1:T(8,128)}, u32[]{:S(2)}, u32[]{:S(2)}) collective-permute-start(f32[4,2,16,16,128]{4,3,2,0,1:T(8,128)} %get-tuple-element.377), channel_id=1, source_target_pairs={{0,4},{1,5},{2,6},{3,7},{4,0},{5,1},{6,2},{7,3},{8,12},{9,13},{10,... | collective-permute-start | bytes 3145736 | tf_op jit(solution)/shard_map/ppermute | solution.py:25
  94.3 298.9 %collective-permute-start.5 = (f32[4,2,16,16,128]{4,3,2,0,1:T(8,128)}, f32[4,2,16,16,128]{4,3,2,0,1:T(8,128)}, u32[]{:S(2)}, u32[]{:S(2)}) collective-permute-start(f32[4,2,16,16,128]{4,3,2,0,1:T(8,128)} %get-tuple-element.379), channel_id=1, source_target_pairs={{0,5},{1,4},{2,7},{3,6},{4,1},{5,0},{6,3},{7,2},{8,13},{9,12},{10,... | collective-permute-start | bytes 3145736 | tf_op jit(solution)/shard_map/ppermute | solution.py:25
  94.3 20.3 %copy-start.5 = (f32[4,2,16,16,128]{4,3,2,0,1:T(8,128)}, f32[4,2,16,16,128]{4,3,2,0,1:T(8,128)S(1)}, u32[]{:S(2)}) copy-start(f32[4,2,16,16,128]{4,3,2,0,1:T(8,128)S(1)} %collective-permute-done.1) | copy-start | bytes 3145732
  94.3 357.0 %collective-permute-start.6 = (f32[4,2,16,16,128]{4,3,2,0,1:T(8,128)}, f32[4,2,16,16,128]{4,3,2,0,1:T(8,128)}, u32[]{:S(2)}, u32[]{:S(2)}) collective-permute-start(f32[4,2,16,16,128]{4,3,2,0,1:T(8,128)} %get-tuple-element.378), channel_id=1, source_target_pairs={{0,6},{1,7},{2,4},{3,5},{4,2},{5,3},{6,0},{7,1},{8,14},{9,15},{10,... | collective-permute-start | bytes 3145736 | tf_op jit(solution)/shard_map/ppermute | solution.py:25
  113.3 396.1 %collective-permute-start.7 = (f32[4,2,16,16,128]{4,3,2,0,1:T(8,128)}, f32[4,2,16,16,128]{4,3,2,0,1:T(8,128)}, u32[]{:S(2)}, u32[]{:S(2)}) collective-permute-start(f32[4,2,16,16,128]{4,3,2,0,1:T(8,128)} %get-tuple-element.372), channel_id=1, source_target_pairs={{0,7},{1,6},{2,5},{3,4},{4,3},{5,2},{6,1},{7,0},{8,15},{9,14},{10,... | collective-permute-start | bytes 3145736 | tf_op jit(solution)/shard_map/ppermute | solution.py:25
  124.0 39.3 %copy-start.6 = (f32[4,2,16,16,128]{4,3,2,0,1:T(8,128)S(1)}, f32[4,2,16,16,128]{4,3,2,0,1:T(8,128)}, u32[]{:S(2)}) copy-start(f32[4,2,16,16,128]{4,3,2,0,1:T(8,128)} %copy-done.5) | copy-start | bytes 3145732
  567.6 6.2 copy-start
  738.9 9.6 copy-start.9
  745.9 2.0 copy-start.3
  748.0 10.0 %collective-permute-start.8 = (f32[4,3,128,128]{2,3,1,0:T(8,128)S(1)}, f32[4,3,128,128]{2,3,1,0:T(8,128)S(1)}, u32[]{:S(2)}, u32[]{:S(2)}) collective-permute-start(f32[4,3,128,128]{2,3,1,0:T(8,128)S(1)} %slice.383), channel_id=1, source_target_pairs={{0,7},{1,0},{2,1},{3,2},{4,3},{5,4},{6,5},{7,6},{8,15},{9,8},{10,9... | collective-permute-start | bytes 2359304 | tf_op jit(solution)/shard_map/ppermute | solution.py:33
  979.4 15.1 %copy-start.10 = (f32[4,3,512]{2,0,1:T(4,128)}, f32[4,3,512]{2,0,1:T(4,128)S(1)}, u32[]{:S(2)}) copy-start(f32[4,3,512]{2,0,1:T(4,128)S(1)} %get-tuple-element.209) | copy-start | bytes 73732
